TPU v7x, 32 devices: a whole 2x2x4 slice. The times are simulated.
32 devices in a mesh: pts: 8 (over z, core), head: 4 (over y, x).
Axes of the slice: x: 2, y: 2, z: 4, core: 2. Of those that a mesh axis runs over, the one named last changes fastest.
Arguments:
- points: bfloat16 [73728, 128], P('pts')
- counts: int32 [8], P('pts'), may hold values from 1 to 9216, 55296 in all
- ln1_gain: float32 [2, 128], replicated, may hold values from 0.5 to 1.5
- ln1_bias: float32 [2, 128], replicated, may hold values from -1.5 to 1.5
- w_in: bfloat16 [2, 128, 128], P(None, None, 'head'), may hold values from -0.5 to 0.5
- w_fx: bfloat16 [2, 128, 128], P(None, None, 'head'), may hold values from -0.5 to 0.5
- w_slice: bfloat16 [2, 32, 32], replicated
- temper: float32 [2, 4], replicated, may hold values from 0.5 to 2
- query_weight: bfloat16 [2, 32, 32], replicated
- key_weight: bfloat16 [2, 32, 32], replicated, may hold values from -1 to 1
- value_weight: bfloat16 [2, 32, 32], replicated, may hold values from -1 to 1
- w_out: bfloat16 [2, 128, 128], P(None, 'head'), may hold values from -1 to 1
- b_out: float32 [2, 128], replicated, may hold values from -1.5 to 1.5
- ln2_gain: float32 [2, 128], replicated, may hold values from 0.5 to 1.5
- ln2_bias: float32 [2, 128], replicated, may hold values from -1.5 to 1.5
- w_up: bfloat16 [2, 128, 512], replicated, may hold values from -0.5 to 0.5
- w_down: bfloat16 [2, 512, 128], replicated, may hold values from -0.25 to 0.25
Outputs:
- features: bfloat16 [73728, 128], P(('pts', 'head'))
Inputs may be any that keep to these rules, and one draw needn't show every extreme that they name: counts[i] live points fill the first slots of shard i; at least one shard is full; they sum to 55296.
All inputs are finite; a program needn't handle non-finite values.
Results may differ from a plain program's by a relative error of at most 0.014.
Values may be sent and summed in bfloat16 or wider, within the bound.
A program may use at most 128 MiB of HBM per device.

v0:
```python
import jax
import jax.numpy as jnp
from jax import lax
from jax.sharding import PartitionSpec as P

DH = 32
M = 32


def layer_norm(value, gain, bias):
    mean = jnp.mean(value, axis=-1, keepdims=True)
    centred = value - mean
    var = jnp.mean(centred * centred, axis=-1, keepdims=True)
    return centred * lax.rsqrt(var + 1e-05) * gain + bias


def slice_attention(token_rows, query_weight, key_weight, value_weight):
    head_parts = lax.Precision.HIGHEST
    query_rows = jnp.einsum(
        "aur,rz->auz", token_rows, query_weight.astype(jnp.float32), precision=head_parts
    )
    slice_keys = jnp.einsum(
        "aur,rz->auz", token_rows, key_weight.astype(jnp.float32), precision=head_parts
    )
    slice_values = jnp.einsum(
        "aur,rz->auz", token_rows, value_weight.astype(jnp.float32), precision=head_parts
    )
    scores = jnp.einsum("hme,hke->hmk", query_rows, slice_keys, precision=head_parts) * DH ** (-0.5)
    attn = jax.nn.softmax(scores, axis=-1)
    return jnp.einsum("hmk,hke->hme", attn, slice_values, precision=head_parts).astype(jnp.bfloat16)


def body(
    points,
    counts,
    ln1_gain,
    ln1_bias,
    w_in,
    w_fx,
    w_slice,
    temper,
    query_weight,
    key_weight,
    value_weight,
    w_out,
    b_out,
    ln2_gain,
    ln2_bias,
    w_up,
    w_down,
):
    groups = lax.axis_size("head")
    rows = points.shape[0] // groups
    first_row = lax.axis_index("head") * rows
    layers = w_in.shape[0]
    full_in = lax.all_gather(w_in, "head", axis=2, tiled=True)
    full_fx = lax.all_gather(w_fx, "head", axis=2, tiled=True)
    full_out = lax.all_gather(w_out, "head", axis=1, tiled=True)
    heads = full_in.shape[2] // DH
    live = (first_row + jnp.arange(rows, dtype=jnp.int32) < counts[0]).astype(jnp.float32)
    current = lax.dynamic_slice_in_dim(points, first_row, rows, 0)
    for layer_index in range(layers):
        normed = layer_norm(
            current.astype(jnp.float32), ln1_gain[layer_index], ln1_bias[layer_index]
        ).astype(jnp.bfloat16)
        mid = jnp.dot(normed, full_in[layer_index], preferred_element_type=jnp.float32).astype(
            jnp.bfloat16
        )
        feats = jnp.dot(normed, full_fx[layer_index], preferred_element_type=jnp.float32).astype(
            jnp.bfloat16
        )
        spread = jnp.kron(jnp.eye(heads, dtype=jnp.bfloat16), w_slice[layer_index])
        logits = jnp.dot(mid, spread, preferred_element_type=jnp.float32)
        logits = logits.reshape(rows, heads, M) / temper[layer_index][None, :, None]
        weights = jax.nn.softmax(logits, axis=-1) * live[:, None, None]
        half_weights = weights.astype(jnp.bfloat16).reshape(rows, heads * M)
        total = jnp.sum(weights, axis=0)
        square = jnp.einsum("rs,rl->sl", half_weights, feats, preferred_element_type=jnp.float32)
        square = square.reshape(heads, M, heads, DH)
        numerator = jnp.stack([square[h, :, h, :] for h in range(heads)])
        numerator, total = lax.psum((numerator, total), ("pts", "head"))
        token_rows = numerator / jnp.maximum(total, 1.0)[..., None]
        mixed_token = slice_attention(
            token_rows,
            query_weight[layer_index],
            key_weight[layer_index],
            value_weight[layer_index],
        )
        wide = jnp.einsum(
            "hmv,hvc->hmc",
            mixed_token,
            full_out[layer_index].reshape(heads, DH, -1),
            preferred_element_type=jnp.float32,
        ).astype(jnp.bfloat16).reshape(heads * M, -1)
        projected = jnp.dot(half_weights, wide, preferred_element_type=jnp.float32)
        after = current.astype(jnp.float32) + projected + b_out[layer_index]
        normed2 = layer_norm(after, ln2_gain[layer_index], ln2_bias[layer_index]).astype(
            jnp.bfloat16
        )
        upper = jax.nn.gelu(
            jnp.dot(normed2, w_up[layer_index], preferred_element_type=jnp.float32)
        ).astype(jnp.bfloat16)
        current = (
            after + jnp.dot(upper, w_down[layer_index], preferred_element_type=jnp.float32)
        ).astype(jnp.bfloat16)
    return current


def solution(mesh):
    placed = (
        P("pts", None),
        P("pts"),
        P(),
        P(),
        P(None, None, "head"),
        P(None, None, "head"),
        P(),
        P(),
        P(),
        P(),
        P(),
        P(None, "head", None),
        P(),
        P(),
        P(),
        P(),
        P(),
    )
    return jax.shard_map(
        body, mesh=mesh, in_specs=placed, out_specs=P(("pts", "head"), None), check_vma=False
    )
```

profile of v0, /device:TPU:0, one launch (start us, length us, event | category | flops | bytes accessed | tf_op | source)
XLA Modules:
  0.0 157.5 jit_solution(5383199505180625222)
XLA Ops:
  0.0 1.7 %copy-done = bf16[9216,128]{1,0:T(8,128)(2,1)S(1)} copy-done((bf16[9216,128]{1,0:T(8,128)(2,1)S(1)}, bf16[9216,128]{1,0:T(8,128)(2,1)}, u32[]{:S(2)}) %copy-start) | copy-done | bytes 2359320
  3.5 0.8 broadcast_multiply_fusion
  4.4 9.7 %all_gather.9 = bf16[2,128,128]{1,2,0:T(8,128)(2,1)S(1)} all-gather(bf16[2,128,32]{1,2,0:T(8,128)(2,1)S(1)} %copy-done.10), channel_id=1, replica_groups=mesh['pts'=8,'head'=4] {'head'}, dimensions={2}, use_global_device_ids=true | all-gather | bytes 81920 | tf_op jit(solution)/shard_map/all_gather | solution.py:56
  14.2 1.9 %fusion.122 = (f32[2304,4]{0,1:T(4,128)S(1)}, f32[2304,4,32]{0,2,1:T(8,128)}) fusion(bf16[4,32,128]{2,1,0:T(8,128)(2,1)S(1)} %bitcast.209, f32[4]{0:T(128)S(1)} %get-tuple-element.28, bf16[2,128,128]{1,2,0:T(8,128)(2,1)S(1)} %all_gather.9, bf16[2304,128]{0,1:T(8,128)(2,1)S(1)} %copy.26, f32[128]{0:T(128)S(1)} %get-tuple-element.34, ...), kind=kOutput, calls=%fused_computation.175 | convolution fusion | flops 153944096 | bytes 1897984 | tf_op jit(solution)/shard_map/sub | solution.py:75
  16.7 1.6 %fusion.57 = f32[4,32]{1,0:T(4,128)S(1)} fusion(f32[2304]{0:T(1024)S(1)} %fusion.83, f32[2304,4,32]{0,2,1:T(8,128)} %get-tuple-element.36, f32[2304,4]{0,1:T(4,128)S(1)} %get-tuple-element.35), kind=kLoop, calls=%fused_computation.77 | loop fusion | flops 884608 | bytes 1226240 | tf_op jit(solution)/shard_map/reduce_sum | solution.py:77
  18.3 8.2 %all_gather.10 = bf16[2,128,128]{1,2,0:T(8,128)(2,1)S(1)} all-gather(bf16[2,128,32]{1,2,0:T(8,128)(2,1)S(1)} %copy-done.11), channel_id=1, replica_groups=mesh['pts'=8,'head'=4] {'head'}, dimensions={2}, use_global_device_ids=true | all-gather | bytes 81920 | tf_op jit(solution)/shard_map/all_gather | solution.py:57
  27.7 40.2 %all-reduce.1 = (f32[4,32,32]{2,1,0:T(8,128)S(1)}, f32[4,32]{1,0:T(4,128)S(1)}) all-reduce(f32[4,32,32]{2,1,0:T(8,128)S(1)} %pad_maximum_fusion, f32[4,32]{1,0:T(4,128)S(1)} %fusion.57), channel_id=1, replica_groups=mesh['pts'=8,'head'=4] {'pts','head'}, use_global_device_ids=true, to_apply=%region_4.5 | all-reduce | flops 4224 | bytes 33792 | tf_op jit(solution)/shard_map/psum | solution.py:81
  69.3 9.0 %all_gather.11 = bf16[2,128,128]{2,1,0:T(8,128)(2,1)S(1)} all-gather(bf16[2,32,128]{2,1,0:T(8,128)(2,1)S(1)} %copy-done.12), channel_id=1, replica_groups=mesh['pts'=8,'head'=4] {'head'}, dimensions={1}, use_global_device_ids=true | all-gather | bytes 81920 | tf_op jit(solution)/shard_map/all_gather | solution.py:58
  79.4 2.8 %fusion.126 = (f32[2304]{0:T(1024)S(1)}, f32[2304,128]{0,1:T(8,128)}) fusion(f32[128]{0:T(128)S(1)} %get-tuple-element.26, bf16[4,32,32]{2,1,0:T(8,128)(2,1)S(1)} %convolution_convert_fusion.7, bf16[4,32,128]{2,1,0:T(8,128)(2,1)S(1)} %bitcast.212, f32[2304]{0:T(1024)S(1)} %fusion.83, f32[2304,4,32]{0,2,1:T(8,128)} %get-tuple-element.36, ...), kind=kOutput, calls=%fused_computation.177 | convolution fusion | flops 78624512 | bytes 3045888 | tf_op jit(solution)/shard_map/dot_general | solution.py:95
  82.2 1.4 multiply_reduce_fusion.2
  84.8 4.6 %fusion.127 = (f32[2304]{0:T(1024)}, f32[2304,128]{0,1:T(8,128)S(1)}) fusion(f32[2304,128]{0,1:T(8,128)} %get-tuple-element.40, bf16[2,512,128]{2,1,0:T(8,128)(2,1)} %param.33, f32[128]{0:T(128)} %get-tuple-element.24, f32[128]{0:T(128)} %get-tuple-element.51, f32[2304]{0:T(1024)} %add_rsqrt_fusion.2, f32[2304]{0:T(1024)} %copy-done.8, ...), kind=kOutput, calls=%fused_computation.178 | convolution fusion | flops 617248512 | bytes 3835904 | tf_op jit(solution)/shard_map/dot_general | solution.py:104
  90.3 1.2 add_convert_fusion.1
  91.5 1.6 %mul.210 = bf16[128,128]{0,1:T(8,128)(2,1)} reshape(bf16[4,32,4,32]{1,0,3,2:T(4,128)(2,1)} %get-tuple-element.29) | data formatting | bytes 65536 | tf_op jit(solution)/shard_map/jit(kron)/mul | solution.py:72
  93.1 3.4 %fusion.130 = (f32[2304,4]{0,1:T(4,128)}, f32[2304,4,32]{0,2,1:T(8,128)}) fusion(bf16[4,32,128]{2,1,0:T(8,128)(2,1)} %bitcast.210, bf16[2304,128]{0,1:T(8,128)(2,1)} %add_convert_fusion.1, f32[4]{0:T(128)S(1)} %get-tuple-element.27, bf16[2,128,128]{1,2,0:T(8,128)(2,1)} %copy-done.7), kind=kOutput, calls=%fused_computation.179 | convolution fusion | flops 152174624 | bytes 1871888 | tf_op jit(solution)/shard_map/sub | solution.py:75
  96.5 1.6 %fusion.59 = f32[4,32]{1,0:T(4,128)S(1)} fusion(f32[2304]{0:T(1024)S(1)} %fusion.83, f32[2304,4,32]{0,2,1:T(8,128)} %get-tuple-element.44, f32[2304,4]{0,1:T(4,128)} %get-tuple-element.43), kind=kLoop, calls=%fused_computation.79 | loop fusion | flops 884608 | bytes 1226240 | tf_op jit(solution)/shard_map/reduce_sum | solution.py:77
  99.7 40.3 %all-reduce = (f32[4,32,32]{2,1,0:T(8,128)}, f32[4,32]{1,0:T(4,128)}) all-reduce(f32[4,32,32]{2,1,0:T(8,128)} %pad_maximum_fusion.1, f32[4,32]{1,0:T(4,128)S(1)} %fusion.59), channel_id=1, replica_groups=mesh['pts'=8,'head'=4] {'pts','head'}, use_global_device_ids=true, to_apply=%region_15.16 | all-reduce | flops 4224 | bytes 33792 | tf_op jit(solution)/shard_map/psum | solution.py:81
  140.7 1.1 fusion.86
  141.8 1.1 fusion.88
  143.1 1.1 fusion.84
  144.2 0.9 convolution_convert_fusion.5
  145.2 3.4 %fusion.132 = (f32[2304]{0:T(1024)}, f32[2304,128]{0,1:T(8,128)}) fusion(f32[128]{0:T(128)} %get-tuple-element.25, f32[2304,128]{0,1:T(8,128)S(1)} %get-tuple-element.42, bf16[4,32,32]{2,1,0:T(8,128)(2,1)} %convolution_convert_fusion.5, bf16[4,32,128]{2,1,0:T(8,128)(2,1)} %bitcast.211, f32[2304]{0:T(1024)S(1)} %fusion.83, ...), kind=kOutput, calls=%fused_computation.181 | convolution fusion | flops 78329600 | bytes 3635712 | tf_op jit(solution)/shard_map/dot_general | solution.py:95
  149.4 1.4 multiply_reduce_fusion
  151.4 4.0 %fusion.27 = bf16[2304,128]{0,1:T(8,128)(2,1)} fusion(f32[2304,128]{0,1:T(8,128)S(1)} %copy-done.4, f32[128]{0:T(128)S(1)} %copy-done.22, f32[128]{0:T(128)} %get-tuple-element.52, f32[2304]{0:T(1024)} %add_rsqrt_fusion, f32[2304]{0:T(1024)S(1)} %broadcast_multiply_fusion.2, bf16[2,512,128]{2,1,0:T(8,128)(2,1)} %param.33, bf16[2,128,512]{2,1,0:T(8,128)(2,1)} %param.32), kind=kOutput, calls=%fused_computation.35 | convolution fusion | flops 616660992 | bytes 3236864 | tf_op jit(solution)/shard_map/dot_general | solution.py:104
  155.4 2.1 %copy.22 = bf16[2304,128]{1,0:T(8,128)(2,1)} copy(bf16[2304,128]{0,1:T(8,128)(2,1)} %fusion.27) | data formatting | bytes 1179648 | tf_op jit(solution)/shard_map/convert_element_type | solution.py:105
  (93 shorter events, 11.4 us)
Async XLA Ops:
  0.0 1.7 %copy-start = (bf16[9216,128]{1,0:T(8,128)(2,1)S(1)}, bf16[9216,128]{1,0:T(8,128)(2,1)}, u32[]{:S(2)}) copy-start(bf16[9216,128]{1,0:T(8,128)(2,1)} %param.17) | copy-start | bytes 7077892
  1.7 1.6 copy-start.13
  2.0 2.4 %copy-start.10 = (bf16[2,128,32]{1,2,0:T(8,128)(2,1)S(1)}, bf16[2,128,32]{1,2,0:T(8,128)(2,1)}, u32[]{:S(2)}) copy-start(bf16[2,128,32]{1,2,0:T(8,128)(2,1)} %param.21) | copy-start | bytes 49156
  2.0 12.1 %copy-start.16 = (f32[2,4]{1,0:T(2,128)S(1)}, f32[2,4]{1,0:T(2,128)}, u32[]{:S(2)}) copy-start(f32[2,4]{1,0:T(2,128)} %param.24) | copy-start | bytes 100
  14.1 1.9 %copy-start.7 = (bf16[2,128,128]{1,2,0:T(8,128)(2,1)}, bf16[2,128,128]{1,2,0:T(8,128)(2,1)S(1)}, u32[]{:S(2)}) copy-start(bf16[2,128,128]{1,2,0:T(8,128)(2,1)S(1)} %all_gather.9) | copy-start | bytes 196612
  16.0 2.3 %copy-start.11 = (bf16[2,128,32]{1,2,0:T(8,128)(2,1)S(1)}, bf16[2,128,32]{1,2,0:T(8,128)(2,1)}, u32[]{:S(2)}) copy-start(bf16[2,128,32]{1,2,0:T(8,128)(2,1)} %param.22) | copy-start | bytes 49156
  16.7 10.3 %copy-start.2 = (f32[2304,4,32]{0,2,1:T(8,128)S(1)}, f32[2304,4,32]{0,2,1:T(8,128)}, u32[]{:S(2)}) copy-start(f32[2304,4,32]{0,2,1:T(8,128)} %get-tuple-element.36) | copy-start | bytes 3538948
  26.5 1.1 copy-start.5
  27.0 40.9 %copy-start.23 = (bf16[2,32,32]{2,1,0:T(8,128)(2,1)S(1)}, bf16[2,32,32]{2,1,0:T(8,128)(2,1)}, u32[]{:S(2)}) copy-start(bf16[2,32,32]{2,1,0:T(8,128)(2,1)} %param.26) | copy-start | bytes 12292
  27.0 41.2 %copy-start.24 = (bf16[2,32,32]{2,1,0:T(8,128)(2,1)S(1)}, bf16[2,32,32]{2,1,0:T(8,128)(2,1)}, u32[]{:S(2)}) copy-start(bf16[2,32,32]{2,1,0:T(8,128)(2,1)} %param.25) | copy-start | bytes 12292
  27.0 41.7 %copy-start.25 = (bf16[2,32,32]{2,1,0:T(8,128)(2,1)S(1)}, bf16[2,32,32]{2,1,0:T(8,128)(2,1)}, u32[]{:S(2)}) copy-start(bf16[2,32,32]{2,1,0:T(8,128)(2,1)} %param.27) | copy-start | bytes 12292
  27.6 41.6 %copy-start.12 = (bf16[2,32,128]{2,1,0:T(8,128)(2,1)S(1)}, bf16[2,32,128]{2,1,0:T(8,128)(2,1)}, u32[]{:S(2)}) copy-start(bf16[2,32,128]{2,1,0:T(8,128)(2,1)} %param.28) | copy-start | bytes 49156
  27.6 51.2 %copy-start.17 = (f32[2,128]{1,0:T(2,128)S(1)}, f32[2,128]{1,0:T(2,128)}, u32[]{:S(2)}) copy-start(f32[2,128]{1,0:T(2,128)} %param.29) | copy-start | bytes 3076
  82.2 2.1 %copy-start.20 = (f32[2,128]{1,0:T(2,128)S(1)}, f32[2,128]{1,0:T(2,128)}, u32[]{:S(2)}) copy-start(f32[2,128]{1,0:T(2,128)} %param.31) | copy-start | bytes 3076
  82.2 2.1 %copy-start.21 = (f32[2,128]{1,0:T(2,128)S(1)}, f32[2,128]{1,0:T(2,128)}, u32[]{:S(2)}) copy-start(f32[2,128]{1,0:T(2,128)} %param.30) | copy-start | bytes 3076
  82.2 2.7 %copy-start.8 = (f32[2304]{0:T(1024)}, f32[2304]{0:T(1024)S(1)}, u32[]{:S(2)}) copy-start(f32[2304]{0:T(1024)S(1)} %broadcast_multiply_fusion.4) | copy-start | bytes 27652
  89.4 0.9 copy-start.14
  89.4 0.9 copy-start.15
  96.5 1.6 %copy-start.1 = (bf16[2304,128]{0,1:T(8,128)(2,1)S(1)}, bf16[2304,128]{0,1:T(8,128)(2,1)}, u32[]{:S(2)}) copy-start(bf16[2304,128]{0,1:T(8,128)(2,1)} %add_convert_fusion.1) | copy-start | bytes 1769476
  96.5 1.6 %copy-start.6 = (bf16[2,128,128]{1,2,0:T(8,128)(2,1)S(1)}, bf16[2,128,128]{1,2,0:T(8,128)(2,1)}, u32[]{:S(2)}) copy-start(bf16[2,128,128]{1,2,0:T(8,128)(2,1)} %copy-done.5) | copy-start | bytes 196612
  96.5 2.0 %copy-start.3 = (f32[2304,4,32]{0,2,1:T(8,128)S(1)}, f32[2304,4,32]{0,2,1:T(8,128)}, u32[]{:S(2)}) copy-start(f32[2304,4,32]{0,2,1:T(8,128)} %get-tuple-element.44) | copy-start | bytes 3538948
  96.5 2.0 %copy-start.9 = (f32[2304,4]{0,1:T(4,128)S(1)}, f32[2304,4]{0,1:T(4,128)}, u32[]{:S(2)}) copy-start(f32[2304,4]{0,1:T(4,128)} %get-tuple-element.43) | copy-start | bytes 110596
  148.6 2.8 %copy-start.4 = (f32[2304,128]{0,1:T(8,128)S(1)}, f32[2304,128]{0,1:T(8,128)}, u32[]{:S(2)}) copy-start(f32[2304,128]{0,1:T(8,128)} %get-tuple-element.48) | copy-start | bytes 3538948
  148.6 2.8 %copy-start.22 = (f32[128]{0:T(128)S(1)}, f32[128]{0:T(128)}, u32[]{:S(2)}) copy-start(f32[128]{0:T(128)} %get-tuple-element.23) | copy-start | bytes 1540
  (2 other events, 1.4 us)
where the time goes:
time: 159 us; the launch traced here: 158 us
  blocking collectives  107 us (67%)
  matrix products  27.6 us (17%)
  other arithmetic  12.6 us (8%)
  local copies, waits for them, and re-layouts  8.79 us (6%)
    psum x2, blocking collectives, body(): numerator, total = lax.psum((numerator, total), ('pts', 'head'))  80.5 us
    all_gather x1, blocking collectives, body(): full_in = lax.all_gather(w_in, 'head', axis=2, tiled=True)  9.72 us
    all_gather x1, blocking collectives, body(): full_out = lax.all_gather(w_out, 'head', axis=1, tiled=True)  9 us
    dot_general x2, matrix products, body(): jnp.dot(upper, w_down[layer_index], preferred_element_type=jnp.float32)  8.51 us
    all_gather x1, blocking collectives, body(): full_fx = lax.all_gather(w_fx, 'head', axis=2, tiled=True)  8.21 us
    dot_general x2, matrix products, body(): projected = jnp.dot(half_weights, wide, preferred_element_type=jnp.float32)  6.22 us
    sub x2, matrix products, body(): weights = jax.nn.softmax(logits, axis=-1) * live[:, None, None]  5.29 us
    reduce_sum x2, other arithmetic, body(): total = jnp.sum(weights, axis=0)  3.22 us

commit v1 on v0

v1 whole, which is shorter than its diff:
```python
import functools
import math

import jax
import jax.numpy as jnp
from jax import lax
from jax.experimental import pallas as pl
from jax.experimental.pallas import tpu as pltpu
from jax.sharding import PartitionSpec as P

DH = 32
M = 32
TILE = 768
MESH = pl.DeviceIdType.MESH
HIGH = lax.Precision.HIGHEST
F32 = jnp.float32
BF16 = jnp.bfloat16
NT = (((1,), (1,)), ((), ()))


def norm_columns(value, gain, bias):
    mean = jnp.mean(value, axis=0, keepdims=True)
    centred = value - mean
    var = jnp.mean(centred * centred, axis=0, keepdims=True)
    return centred * lax.rsqrt(var + 1e-05) * gain + bias


def kernel(
    groups,
    shards,
    rows,
    tiles,
    counts,
    temper,
    points,
    ln1_gain,
    ln1_bias,
    w_in,
    w_fx,
    w_slice,
    query_weight,
    key_weight,
    value_weight,
    w_out,
    b_out,
    ln2_gain,
    ln2_bias,
    w_up,
    w_down,
    out,
    x_rows,
    x_cols,
    normed_ref,
    weights_ref,
    wl_ref,
    up_t,
    down_t,
    fx_pad,
    par,
    par_cols,
    sums,
    recv_a,
    own_b,
    recv_b,
    g_ref,
    row_sem,
    wl_send,
    wl_recv,
    a_send,
    a_recv,
    b_send,
    b_recv,
    c_send,
    c_recv,
):
    layers, _, width = w_in.shape
    spread = groups * M
    hd = lax.axis_index("head")
    pt = lax.axis_index("pts")

    def head_peer(k):
        return lax.rem(hd + k, groups)

    def pts_peer(k):
        return lax.rem(pt + k, shards)

    barrier = pltpu.get_barrier_semaphore()
    for k in range(1, groups):
        pl.semaphore_signal(barrier, inc=1, device_id={"head": head_peer(k)}, device_id_type=MESH)
    for k in range(1, shards):
        pl.semaphore_signal(barrier, inc=1, device_id={"pts": pts_peer(k)}, device_id_type=MESH)
    first = pl.multiple_of(hd * rows, 64)
    load = pltpu.make_async_copy(
        points.at[pl.ds(first, rows)], x_rows.at[pl.ds(0, rows)], row_sem
    )
    load.start()

    own_head = pl.ds(pl.multiple_of(hd * M, M), M)
    for l in range(layers):
        scale = jnp.full((M, width), temper[l, hd], F32)
        w_head = w_in[l].astype(F32)
        slicer = w_slice[l].astype(F32).T
        folded = jnp.dot(slicer, w_head, preferred_element_type=F32, precision=HIGH)
        wl_ref[l, own_head, :] = (folded * math.log2(math.e) / scale).astype(BF16)
    pl.semaphore_wait(barrier, groups + shards - 2)

    wl_copies = []
    for k in range(1, groups):
        for l in range(layers):
            copy = pltpu.make_async_remote_copy(
                src_ref=wl_ref.at[l, own_head],
                dst_ref=wl_ref.at[l, own_head],
                send_sem=wl_send.at[l, k],
                recv_sem=wl_recv.at[l, k],
                device_id={"head": head_peer(k)},
                device_id_type=MESH,
            )
            copy.start()
            wl_copies.append(copy)

    par[...] = jnp.zeros_like(par)
    for i, ref in enumerate((ln1_gain, ln1_bias, b_out, ln2_gain, ln2_bias)):
        par[i * layers : (i + 1) * layers, :] = ref[...]
    par_t = par[...].T
    for i in range(5 * layers):
        par_cols[i] = jnp.broadcast_to(par_t[:, i : i + 1], (width, TILE))
    fx_pad[...] = jnp.zeros_like(fx_pad)
    for l in range(layers):
        fx_pad[l, :DH, :] = w_fx[l].astype(F32)
    if tiles * TILE > rows:
        x_rows[rows:, :] = jnp.zeros((tiles * TILE - rows, width), BF16)
    load.wait()

    def param(i, l):
        return par_cols[i * layers + l]

    def first_half(l, t, normed):
        logits = jnp.dot(wl_ref[l], normed, preferred_element_type=F32)
        logits = logits.reshape(groups, M, TILE)
        top = jnp.max(logits, axis=1, keepdims=True)
        grown = jnp.exp2(logits - top)
        index = t * TILE + lax.broadcasted_iota(jnp.int32, (1, 1, TILE), 2)
        live = jnp.logical_and(index < rows, index + hd * rows < counts[0]).astype(F32)
        weights = grown * (live / jnp.sum(grown, axis=1, keepdims=True))
        half = weights.reshape(spread, TILE).astype(BF16)
        weights_ref[t] = half
        both = jnp.concatenate([normed, jnp.ones((128, TILE), BF16)], axis=0)
        sums[l] += lax.dot_general(half, both, NT, preferred_element_type=F32)

    def second_half(l, t, g_t):
        x = x_cols[t].astype(F32)
        after = x + jnp.dot(g_t, weights_ref[t], preferred_element_type=F32) + param(2, l)
        normed = norm_columns(after, param(3, l), param(4, l)).astype(BF16)
        upper = jnp.dot(up_t[l], normed, preferred_element_type=F32)
        inner = upper * (0.7978845608028654 + 0.035677408136300125 * (upper * upper))
        half = 0.5 * upper
        upper = (half + half * jnp.tanh(inner)).astype(BF16)
        return (after + jnp.dot(down_t[l], upper, preferred_element_type=F32)).astype(BF16)

    def exchange(l):
        copies = []
        for k in range(1, groups):
            copy = pltpu.make_async_remote_copy(
                src_ref=sums.at[l, pl.ds(pl.multiple_of(head_peer(k) * M, M), M)],
                dst_ref=recv_a.at[l, k],
                send_sem=a_send.at[l, k],
                recv_sem=a_recv.at[l, k],
                device_id={"head": head_peer(k)},
                device_id_type=MESH,
            )
            copy.start()
            copies.append(copy)
        up_t[l] = w_up[l].astype(F32).T.astype(BF16)
        down_t[l] = w_down[l].astype(F32).T.astype(BF16)
        for copy in copies:
            copy.wait()
        square = sums[l, own_head, :]
        for k in range(1, groups):
            square = square + recv_a[l, k]
        numer = lax.dot_general(
            square[:, :width], fx_pad[l], NT, preferred_element_type=F32, precision=HIGH
        )
        lane = lax.broadcasted_iota(jnp.int32, (M, 128), 1)
        own_b[l] = jnp.where(lane < DH, numer, square[:, width:])
        copies = []
        for k in range(1, shards):
            copy = pltpu.make_async_remote_copy(
                src_ref=own_b.at[l],
                dst_ref=recv_b.at[l, k],
                send_sem=b_send.at[l, k],
                recv_sem=b_recv.at[l, k],
                device_id={"pts": pts_peer(k)},
                device_id_type=MESH,
            )
            copy.start()
            copies.append(copy)
        for copy in copies:
            copy.wait()
        summed = own_b[l]
        for k in range(1, shards):
            summed = summed + recv_b[l, k]
        token = summed[:, :DH] / jnp.maximum(summed[:, 127:128], 1.0)
        query = jnp.dot(token, query_weight[l].astype(F32), preferred_element_type=F32, precision=HIGH)
        keys = jnp.dot(token, key_weight[l].astype(F32), preferred_element_type=F32, precision=HIGH)
        value = jnp.dot(token, value_weight[l].astype(F32), preferred_element_type=F32, precision=HIGH)
        scores = lax.dot_general(query, keys, NT, preferred_element_type=F32, precision=HIGH)
        attn = jax.nn.softmax(scores * DH ** (-0.5), axis=-1)
        mixed = jnp.dot(attn, value, preferred_element_type=F32, precision=HIGH).astype(BF16)
        wide = jnp.dot(mixed, w_out[l], preferred_element_type=F32)
        g_ref[l, own_head, :] = wide.astype(BF16)
        copies = []
        for k in range(1, groups):
            copy = pltpu.make_async_remote_copy(
                src_ref=g_ref.at[l, own_head],
                dst_ref=g_ref.at[l, own_head],
                send_sem=c_send.at[l, k],
                recv_sem=c_recv.at[l, k],
                device_id={"head": head_peer(k)},
                device_id_type=MESH,
            )
            copy.start()
            copies.append(copy)
        for copy in copies:
            copy.wait()
        return g_ref[l].astype(F32).T.astype(BF16)

    sums[...] = jnp.zeros_like(sums)

    @pl.loop(0, tiles)
    def _(t):
        at = pl.ds(pl.multiple_of(t * TILE, TILE), TILE)
        x = x_rows[at, :].astype(F32).T
        x_cols[t] = x.astype(BF16)
        normed_ref[t] = norm_columns(x, param(0, 0), param(1, 0)).astype(BF16)

    for copy in wl_copies:
        copy.wait()

    @pl.loop(0, tiles)
    def _(t):
        first_half(0, t, normed_ref[t])

    for l in range(layers):
        g_t = exchange(l)

        @pl.loop(0, tiles)
        def _(t, l=l, g_t=g_t):
            x = second_half(l, t, g_t)
            if l < layers - 1:
                x_cols[t] = x
                normed = norm_columns(x.astype(F32), param(0, l + 1), param(1, l + 1))
                first_half(l + 1, t, normed.astype(BF16))
            else:
                at = pl.ds(pl.multiple_of(t * TILE, TILE), TILE)
                x_rows[at, :] = x.astype(F32).T.astype(BF16)

    store = pltpu.make_async_copy(x_rows.at[pl.ds(0, rows)], out, row_sem)
    store.start()
    store.wait()


def body(
    points,
    counts,
    ln1_gain,
    ln1_bias,
    w_in,
    w_fx,
    w_slice,
    temper,
    query_weight,
    key_weight,
    value_weight,
    w_out,
    b_out,
    ln2_gain,
    ln2_bias,
    w_up,
    w_down,
):
    groups = lax.axis_size("head")
    shards = lax.axis_size("pts")
    rows = points.shape[0] // groups
    layers, width, part = w_in.shape
    assert part == DH
    hidden = w_up.shape[2]
    spread = groups * M
    tiles = -(-rows // TILE)
    vmem = pl.BlockSpec(memory_space=pltpu.VMEM)
    smem = pl.BlockSpec(memory_space=pltpu.SMEM)
    hbm = pl.BlockSpec(memory_space=pl.ANY)
    dma = pltpu.SemaphoreType.DMA
    return pl.pallas_call(
        functools.partial(kernel, groups, shards, rows, tiles),
        out_shape=jax.ShapeDtypeStruct((rows, width), BF16),
        in_specs=[smem, smem, hbm] + [vmem] * 14,
        out_specs=hbm,
        scratch_shapes=[
            pltpu.VMEM((tiles * TILE, width), BF16),
            pltpu.VMEM((tiles, width, TILE), BF16),
            pltpu.VMEM((tiles, width, TILE), BF16),
            pltpu.VMEM((tiles, spread, TILE), BF16),
            pltpu.VMEM((layers, spread, width), BF16),
            pltpu.VMEM((layers, hidden, width), BF16),
            pltpu.VMEM((layers, width, hidden), BF16),
            pltpu.VMEM((layers, 128, width), F32),
            pltpu.VMEM((-(-5 * layers // 8) * 8, width), F32),
            pltpu.VMEM((5 * layers, width, TILE), F32),
            pltpu.VMEM((layers, spread, width + 128), F32),
            pltpu.VMEM((layers, groups, M, width + 128), F32),
            pltpu.VMEM((layers, M, 128), F32),
            pltpu.VMEM((layers, shards, M, 128), F32),
            pltpu.VMEM((layers, spread, width), BF16),
            dma,
            dma((layers, groups)),
            dma((layers, groups)),
            dma((layers, groups)),
            dma((layers, groups)),
            dma((layers, shards)),
            dma((layers, shards)),
            dma((layers, groups)),
            dma((layers, groups)),
        ],
        compiler_params=pltpu.CompilerParams(collective_id=0, has_side_effects=True),
    )(
        counts,
        temper,
        points,
        ln1_gain,
        ln1_bias,
        w_in.swapaxes(1, 2),
        w_fx.swapaxes(1, 2),
        w_slice,
        query_weight,
        key_weight,
        value_weight,
        w_out,
        b_out,
        ln2_gain,
        ln2_bias,
        w_up,
        w_down,
    )


def solution(mesh):
    placed = (
        P("pts", None),
        P("pts"),
        P(),
        P(),
        P(None, None, "head"),
        P(None, None, "head"),
        P(),
        P(),
        P(),
        P(),
        P(),
        P(None, "head", None),
        P(),
        P(),
        P(),
        P(),
        P(),
    )
    return jax.shard_map(
        body, mesh=mesh, in_specs=placed, out_specs=P(("pts", "head"), None), check_vma=False
    )
```

time: 159 us -> 48.1 us (0.30)
  blocking collectives: 107 us -> 0 us
  Pallas kernels: 0 us -> 45.3 us
  matrix products: 27.6 us -> 0 us
  other arithmetic: 12.6 us -> 0 us
  local copies, waits for them, and re-layouts: 8.79 us -> 1.92 us
    psum x2 -> x0, blocking collectives: 80.5 us -> none  [body(): numerator, total = lax.psum((numerator, total), ('pts', 'head'))]
    pallas_call x0 -> x1, Pallas kernels: none -> 45.3 us  [body(): pl.pallas_call(functools.partial(kernel, groups, shards, rows, tiles), ou...]
    all_gather x3 -> x0, blocking collectives: 26.9 us -> none  [the longest x1 9.72 us: body(): full_in = lax.all_gather(w_in, 'head', axis=2, tiled=True)]
    dot_general x18 -> x0, matrix products: 22.3 us -> none  [the longest x2 8.51 us: body(): jnp.dot(upper, w_down[layer_index], preferred_element_type=jnp.float32)]
    reduce_sum x9 -> x0, other arithmetic: 6.53 us -> none  [the longest x2 3.22 us: body(): total = jnp.sum(weights, axis=0)]
    sub x2 -> x0, matrix products: 5.29 us -> none  [body(): weights = jax.nn.softmax(logits, axis=-1) * live[:, None, None]]
    convert_element_type x1 -> x0, local copies, waits for them, and re-layouts: 2.12 us -> none  [body(): current = (after + jnp.dot(upper, w_down[layer_index], preferred_element_...]
    mul x5 -> x0, local copies, waits for them, and re-layouts: 1.94 us -> none  [body(): spread = jnp.kron(jnp.eye(heads, dtype=jnp.bfloat16), w_slice[layer_index])]
where the time goes in v1:
time: 48.1 us; the launch traced here: 47.9 us
  Pallas kernels  45.3 us (94%)
  local copies, waits for them, and re-layouts  1.92 us (4%)
  between operations  0.66 us (1%)
    pallas_call x1, Pallas kernels, body(): pl.pallas_call(functools.partial(kernel, groups, shards, rows, tiles), ou...  45.3 us
    unnamed x1, local copies, waits for them, and re-layouts  1.92 us

profile of v1, /device:TPU:0, one launch (start us, length us, event | category | flops | bytes accessed | tf_op | source)
XLA Modules:
  0.0 47.9 jit_solution(10054373902235845461)
XLA Ops:
  0.7 45.3 %shard_map.163 = bf16[2304,128]{1,0:T(8,128)(2,1)} custom-call(s32[1]{0:T(128)S(6)} %copy.19.counts, f32[2,4]{1,0:T(2,128)} %temper.1, bf16[9216,128]{1,0:T(8,128)(2,1)} %points.1, f32[2,128]{1,0:T(2,128)} %ln1_gain.1, f32[2,128]{1,0:T(2,128)} %ln1_bias.1, bf16[2,32,128]{2,1,0:T(8,128)(2,1)} %bitcast.2, bf16[2,32,128]{2,1,0:T(8,128)(2,1)} %bitcast.3, ...), custom_call_target="tpu_custom_call" | custom-call | tf_op jit(solution)/shard_map/pallas_call | solution.py:293
  46.0 1.9 %copy.20 = bf16[2304,128]{1,0:T(8,128)(2,1)} copy(bf16[2304,128]{1,0:T(8,128)(2,1)} %shard_map.163) | data formatting | bytes 1179648

commit v2 on v1

--- a/solution.py
+++ b/solution.py
@@ -55,14 +55,17 @@
     wl_ref,
     up_t,
     down_t,
-    fx_pad,
+    fx_all,
+    out_all,
     par,
     par_cols,
     sums,
+    pay,
     recv_a,
     own_b,
     recv_b,
-    g_ref,
+    joined,
+    maps,
     row_sem,
     wl_send,
     wl_recv,
@@ -84,9 +87,16 @@
     def pts_peer(k):
         return lax.rem(pt + k, shards)
 
+    half_m = M // 2
+    core = lax.rem(pt, 2)
+    near = [(k, j) for k in range(groups) for j in range(2) if k or j]
+
+    def near_id(k, j):
+        return {"head": head_peer(k), "pts": pt - core + lax.rem(core + j, 2)}
+
     barrier = pltpu.get_barrier_semaphore()
-    for k in range(1, groups):
-        pl.semaphore_signal(barrier, inc=1, device_id={"head": head_peer(k)}, device_id_type=MESH)
+    for k, j in near:
+        pl.semaphore_signal(barrier, inc=1, device_id=near_id(k, j), device_id_type=MESH)
     for k in range(1, shards):
         pl.semaphore_signal(barrier, inc=1, device_id={"pts": pts_peer(k)}, device_id_type=MESH)
     first = pl.multiple_of(hd * rows, 64)
@@ -102,7 +112,7 @@
         slicer = w_slice[l].astype(F32).T
         folded = jnp.dot(slicer, w_head, preferred_element_type=F32, precision=HIGH)
         wl_ref[l, own_head, :] = (folded * math.log2(math.e) / scale).astype(BF16)
-    pl.semaphore_wait(barrier, groups + shards - 2)
+    pl.semaphore_wait(barrier, 2 * groups + shards - 2)
 
     wl_copies = []
     for k in range(1, groups):
@@ -117,6 +127,19 @@
             )
             copy.start()
             wl_copies.append(copy)
+        for i, (mine, everyone) in enumerate(((w_fx, fx_all), (w_out, out_all))):
+            copy = pltpu.make_async_remote_copy(
+                src_ref=mine,
+                dst_ref=everyone.at[:, own_head],
+                send_sem=c_send.at[i, k],
+                recv_sem=c_recv.at[i, k],
+                device_id={"head": head_peer(k)},
+                device_id_type=MESH,
+            )
+            copy.start()
+            wl_copies.append(copy)
+    fx_all[:, own_head, :] = w_fx[...]
+    out_all[:, own_head, :] = w_out[...]
 
     par[...] = jnp.zeros_like(par)
     for i, ref in enumerate((ln1_gain, ln1_bias, b_out, ln2_gain, ln2_bias)):
@@ -124,9 +147,6 @@
     par_t = par[...].T
     for i in range(5 * layers):
         par_cols[i] = jnp.broadcast_to(par_t[:, i : i + 1], (width, TILE))
-    fx_pad[...] = jnp.zeros_like(fx_pad)
-    for l in range(layers):
-        fx_pad[l, :DH, :] = w_fx[l].astype(F32)
     if tiles * TILE > rows:
         x_rows[rows:, :] = jnp.zeros((tiles * TILE - rows, width), BF16)
     load.wait()
@@ -158,30 +178,61 @@
         return (after + jnp.dot(down_t[l], upper, preferred_element_type=F32)).astype(BF16)
 
     def exchange(l):
+        heads_of_lane = lax.broadcasted_iota(jnp.int32, (M, spread), 1) >> 5
+        square = lax.dot_general(
+            sums[l, :, :width],
+            fx_all[l].astype(F32),
+            NT,
+            preferred_element_type=F32,
+            precision=HIGH,
+        )
+        numer = jnp.zeros((M, spread), F32)
+        total = jnp.zeros((M, spread), F32)
+        for h in range(groups):
+            here = heads_of_lane == h
+            block = slice(h * M, (h + 1) * M)
+            numer = jnp.where(here, square[block], numer)
+            total = jnp.where(here, sums[l, block, width : width + 1], total)
+        for c in range(2):
+            cut = slice(c * half_m, (c + 1) * half_m)
+            pay[l, c, :half_m, :] = numer[cut].astype(BF16)
+            pay[l, c, half_m:, :] = total[cut].astype(BF16)
         copies = []
-        for k in range(1, groups):
+        for k, j in near:
+            target = lax.rem(core + j, 2)
             copy = pltpu.make_async_remote_copy(
-                src_ref=sums.at[l, pl.ds(pl.multiple_of(head_peer(k) * M, M), M)],
-                dst_ref=recv_a.at[l, k],
-                send_sem=a_send.at[l, k],
-                recv_sem=a_recv.at[l, k],
-                device_id={"head": head_peer(k)},
+                src_ref=pay.at[l, target],
+                dst_ref=recv_a.at[l, 2 * k + j],
+                send_sem=a_send.at[l, 2 * k + j],
+                recv_sem=a_recv.at[l, 2 * k + j],
+                device_id=near_id(k, j),
                 device_id_type=MESH,
             )
             copy.start()
             copies.append(copy)
         up_t[l] = w_up[l].astype(F32).T.astype(BF16)
         down_t[l] = w_down[l].astype(F32).T.astype(BF16)
+        same_head = (lax.broadcasted_iota(jnp.int32, (spread, spread), 0) >> 5) == (
+            lax.broadcasted_iota(jnp.int32, (spread, spread), 1) >> 5
+        )
+        across = (
+            (lax.broadcasted_iota(jnp.int32, (DH, spread), 1) & (DH - 1))
+            == lax.broadcasted_iota(jnp.int32, (DH, spread), 0)
+        ).astype(F32).astype(BF16)
+        down = (
+            (lax.broadcasted_iota(jnp.int32, (spread, DH), 0) & (DH - 1))
+            == lax.broadcasted_iota(jnp.int32, (spread, DH), 1)
+        ).astype(F32).astype(BF16)
+        for i, ref in enumerate((query_weight, key_weight, value_weight)):
+            wide = jnp.dot(ref[l], across, preferred_element_type=F32).astype(BF16)
+            full = jnp.dot(down, wide, preferred_element_type=F32)
+            maps[i] = jnp.where(same_head, full, 0.0)
         for copy in copies:
             copy.wait()
-        square = sums[l, own_head, :]
-        for k in range(1, groups):
-            square = square + recv_a[l, k]
-        numer = lax.dot_general(
-            square[:, :width], fx_pad[l], NT, preferred_element_type=F32, precision=HIGH
-        )
-        lane = lax.broadcasted_iota(jnp.int32, (M, 128), 1)
-        own_b[l] = jnp.where(lane < DH, numer, square[:, width:])
+        chip = pay[l, core].astype(F32)
+        for k, j in near:
+            chip = chip + recv_a[l, 2 * k + j].astype(F32)
+        own_b[l] = chip.astype(BF16)
         copies = []
         for k in range(1, shards):
             copy = pltpu.make_async_remote_copy(
@@ -196,33 +247,23 @@
             copies.append(copy)
         for copy in copies:
             copy.wait()
-        summed = own_b[l]
-        for k in range(1, shards):
-            summed = summed + recv_b[l, k]
-        token = summed[:, :DH] / jnp.maximum(summed[:, 127:128], 1.0)
-        query = jnp.dot(token, query_weight[l].astype(F32), preferred_element_type=F32, precision=HIGH)
-        keys = jnp.dot(token, key_weight[l].astype(F32), preferred_element_type=F32, precision=HIGH)
-        value = jnp.dot(token, value_weight[l].astype(F32), preferred_element_type=F32, precision=HIGH)
+        halves = [own_b[l].astype(F32), recv_b[l, 1].astype(F32)]
+        for k in range(2, shards):
+            halves[k % 2] = halves[k % 2] + recv_b[l, k].astype(F32)
+        for j in range(2):
+            at = pl.ds(pl.multiple_of(lax.rem(core + j, 2) * half_m, half_m), half_m)
+            joined[0, at, :] = halves[j][:half_m]
+            joined[1, at, :] = halves[j][half_m:]
+        token = joined[0] / jnp.maximum(joined[1], 1.0)
+        query = jnp.dot(token, maps[0], preferred_element_type=F32, precision=HIGH)
+        keys = jnp.dot(token, maps[1], preferred_element_type=F32, precision=HIGH)
+        value = jnp.dot(token, maps[2], preferred_element_type=F32, precision=HIGH)
+        query = jnp.where(same_head, jnp.concatenate([query] * groups, axis=0), 0.0)
         scores = lax.dot_general(query, keys, NT, preferred_element_type=F32, precision=HIGH)
         attn = jax.nn.softmax(scores * DH ** (-0.5), axis=-1)
-        mixed = jnp.dot(attn, value, preferred_element_type=F32, precision=HIGH).astype(BF16)
-        wide = jnp.dot(mixed, w_out[l], preferred_element_type=F32)
-        g_ref[l, own_head, :] = wide.astype(BF16)
-        copies = []
-        for k in range(1, groups):
-            copy = pltpu.make_async_remote_copy(
-                src_ref=g_ref.at[l, own_head],
-                dst_ref=g_ref.at[l, own_head],
-                send_sem=c_send.at[l, k],
-                recv_sem=c_recv.at[l, k],
-                device_id={"head": head_peer(k)},
-                device_id_type=MESH,
-            )
-            copy.start()
-            copies.append(copy)
-        for copy in copies:
-            copy.wait()
-        return g_ref[l].astype(F32).T.astype(BF16)
+        mixed = jnp.dot(attn, value, preferred_element_type=F32, precision=HIGH)
+        mixed = jnp.where(same_head, mixed, 0.0).astype(BF16)
+        return jnp.dot(mixed, out_all[l], preferred_element_type=F32).T.astype(BF16)
 
     sums[...] = jnp.zeros_like(sums)
 
@@ -303,23 +344,26 @@
             pltpu.VMEM((layers, spread, width), BF16),
             pltpu.VMEM((layers, hidden, width), BF16),
             pltpu.VMEM((layers, width, hidden), BF16),
-            pltpu.VMEM((layers, 128, width), F32),
+            pltpu.VMEM((layers, spread, width), BF16),
+            pltpu.VMEM((layers, spread, width), BF16),
             pltpu.VMEM((-(-5 * layers // 8) * 8, width), F32),
             pltpu.VMEM((5 * layers, width, TILE), F32),
             pltpu.VMEM((layers, spread, width + 128), F32),
-            pltpu.VMEM((layers, groups, M, width + 128), F32),
-            pltpu.VMEM((layers, M, 128), F32),
-            pltpu.VMEM((layers, shards, M, 128), F32),
-            pltpu.VMEM((layers, spread, width), BF16),
+            pltpu.VMEM((layers, 2, M, spread), BF16),
+            pltpu.VMEM((layers, 2 * groups, M, spread), BF16),
+            pltpu.VMEM((layers, M, spread), BF16),
+            pltpu.VMEM((layers, shards, M, spread), BF16),
+            pltpu.VMEM((2, M, spread), F32),
+            pltpu.VMEM((3, spread, spread), F32),
             dma,
             dma((layers, groups)),
             dma((layers, groups)),
-            dma((layers, groups)),
-            dma((layers, groups)),
+            dma((layers, 2 * groups)),
+            dma((layers, 2 * groups)),
             dma((layers, shards)),
             dma((layers, shards)),
-            dma((layers, groups)),
-            dma((layers, groups)),
+            dma((2, groups)),
+            dma((2, groups)),
         ],
         compiler_params=pltpu.CompilerParams(collective_id=0, has_side_effects=True),
     )(

time: 48.1 us -> 41.7 us (0.87)
  Pallas kernels: 45.3 us -> 39 us
    pallas_call x1, Pallas kernels: 45.3 us -> 39 us  [body(): pl.pallas_call(functools.partial(kernel, groups, shards, rows, tiles), ou...]
where the time goes in v2:
time: 41.7 us; the launch traced here: 41.5 us
  Pallas kernels  39 us (94%)
  local copies, waits for them, and re-layouts  1.92 us (5%)
  between operations  0.66 us (2%)
    pallas_call x1, Pallas kernels, body(): pl.pallas_call(functools.partial(kernel, groups, shards, rows, tiles), ou...  39 us
    unnamed x1, local copies, waits for them, and re-layouts  1.92 us

profile of v2, /device:TPU:0, one launch (start us, length us, event | category | flops | bytes accessed | tf_op | source)
XLA Modules:
  0.0 41.5 jit_solution(4840753671832409409)
XLA Ops:
  0.7 39.0 %shard_map.163 = bf16[2304,128]{1,0:T(8,128)(2,1)} custom-call(s32[1]{0:T(128)S(6)} %copy.19.counts, f32[2,4]{1,0:T(2,128)} %temper.1, bf16[9216,128]{1,0:T(8,128)(2,1)} %points.1, f32[2,128]{1,0:T(2,128)} %ln1_gain.1, f32[2,128]{1,0:T(2,128)} %ln1_bias.1, bf16[2,32,128]{2,1,0:T(8,128)(2,1)} %bitcast.2, bf16[2,32,128]{2,1,0:T(8,128)(2,1)} %bitcast.3, ...), custom_call_target="tpu_custom_call" | custom-call | tf_op jit(solution)/shard_map/pallas_call | solution.py:334
  39.6 1.9 %copy.20 = bf16[2304,128]{1,0:T(8,128)(2,1)} copy(bf16[2304,128]{1,0:T(8,128)(2,1)} %shard_map.163) | data formatting | bytes 1179648
